TPU v7x, 32 devices: a whole 2x2x4 slice. The times are simulated.
32 devices in a mesh: parts: 2 (over y), dp: 8 (over z, x), tensor: 2 (over core).
Axes of the slice: x: 2, y: 2, z: 4, core: 2. Of those that a mesh axis runs over, the one named last changes fastest.
Arguments:
- normed: bfloat16 [16, 256, 4096], P(('parts', 'dp')), parts along dimension 0, may hold values from -28 to 28
- q_weight: bfloat16 [4096, 2048], P('dp', 'tensor'), may hold values from -0.09375 to 0.09375
- kv_weight: bfloat16 [4096, 2, 512], P('dp', None, 'tensor'), may hold values from -0.09375 to 0.09375
- o_weight: bfloat16 [2048, 4096], P('tensor', 'dp'), may hold values from -0.5 to 0.5
- lengths: int32 [16], P(('parts', 'dp')), parts along dimension 0, may hold values from 64 to 256
- destinations: int32 [16], P(('parts', 'dp')), parts along dimension 0, may hold values from 0 to 7, each once
Outputs:
- projected: bfloat16 [16, 256, 4096], P(('parts', 'dp'), None, 'tensor'), parts along dimension 0
- kv_cache: bfloat16 [16, 2, 4, 256, 128], P(('parts', 'dp'), None, None, 'tensor'), parts along dimension 0
There are 2 independent parts, one for each index of `parts`. A program takes and returns all parts, laid end to end along the dimension named above; an argument that names none is the same for every part. Nothing has to cross between parts.
All inputs are finite; a program needn't handle non-finite values.
Results may differ from a plain program's by a relative error of at most 0.012.
The roundings to bfloat16 on the way count: a program that leaves them out, or rounds other values in their place, can miss the bound.
Values may be sent and summed in bfloat16 or wider, within the bound.
A program may use at most 128 MiB of HBM per device.

v0:
```python
import math

import jax
import jax.numpy as jnp
from jax import lax
from jax.sharding import PartitionSpec as P

HD = 128


ROPE_BASE = 500000.0


def rotate(values, positions):
    half = values.shape[-1] // 2
    steps = jnp.arange(half, dtype=jnp.float32) * (2.0 / values.shape[-1])
    freq = jnp.power(jnp.float32(ROPE_BASE), -steps)
    angle = positions.astype(jnp.float32)[:, None] * freq[None, :]
    cosine = jnp.cos(angle)[:, None, :]
    sine = jnp.sin(angle)[:, None, :]
    first = values[..., :half]
    second = values[..., half:]
    return jnp.concatenate(
        [first * cosine - second * sine, second * cosine + first * sine], axis=-1
    )


def attend(queries, keys, values, length):
    total = keys.shape[1]
    block = min(total, 512)
    count = total // block
    key_pos = jnp.arange(total, dtype=jnp.int32)

    def one_block(index):
        start = index * block
        scores = jnp.einsum(
            "kgqd,ktd->kgqt", queries, keys, preferred_element_type=jnp.float32
        ) / math.sqrt(HD)
        query_pos = start + jnp.arange(block, dtype=jnp.int32)
        allowed = (query_pos[:, None] >= key_pos[None, :]) & (key_pos[None, :] < length)
        scores = jnp.where(allowed, scores, -jnp.inf)
        peak = jnp.max(scores, axis=-1, keepdims=True)
        expo = jnp.exp(scores - peak)
        weights = (expo / jnp.sum(expo, axis=-1, keepdims=True)).astype(jnp.bfloat16)
        return jnp.einsum(
            "kgqt,ktd->kgqd", weights, values, preferred_element_type=jnp.float32
        ).astype(jnp.bfloat16)

    blocks = lax.map(one_block, jnp.arange(count, dtype=jnp.int32))
    return blocks.transpose(0, 3, 1, 2, 4).reshape(total, -1)


def regroup(cache):
    return lax.all_to_all(cache, "tensor", split_axis=2, concat_axis=1, tiled=True)


def deliver(cache, destination):
    count = lax.axis_size("dp")
    flat = cache.reshape(count, -1)
    sent_to = lax.all_gather(destination, "dp", axis=0, tiled=True)
    spread = lax.all_to_all(flat, "dp", split_axis=0, concat_axis=0, tiled=True)
    slots = jnp.arange(count, dtype=jnp.int32)
    match = sent_to[None, :] == slots[:, None]
    source = jnp.sum(jnp.where(match, slots[None, :], 0), axis=1)
    outgoing = jnp.take(spread, source, axis=0)
    arrived = lax.all_to_all(outgoing, "dp", split_axis=0, concat_axis=0, tiled=True)
    return arrived.reshape(cache.shape)


def on_device(normed, q_weight, kv_weight, o_weight, lengths, destinations):
    tokens = normed[0]
    total = tokens.shape[0]
    q_local = q_weight.shape[1] // HD
    kv_local = kv_weight.shape[2] // HD
    group = q_local // kv_local
    q_full, kv_full = (
        lax.all_gather(q_weight, "dp", axis=0, tiled=True),
        lax.all_gather(kv_weight, "dp", axis=0, tiled=True),
    )
    query_raw = jnp.dot(tokens, q_full, preferred_element_type=jnp.float32)
    pair_raw = jnp.dot(
        tokens, kv_full.reshape(kv_full.shape[0], -1), preferred_element_type=jnp.float32
    )
    positions = jnp.arange(total, dtype=jnp.int32)
    query = rotate(query_raw.reshape(total, q_local, HD), positions).astype(jnp.bfloat16)
    pair = pair_raw.reshape(total, 2, kv_local, HD)
    keys = rotate(pair[:, 0], positions).astype(jnp.bfloat16)
    values = pair[:, 1].astype(jnp.bfloat16)
    grouped = query.reshape(total, kv_local, group, HD).transpose(1, 2, 0, 3)
    key_rows = keys.transpose(1, 0, 2)
    value_rows = values.transpose(1, 0, 2)
    length = lengths[0]
    attended = attend(grouped, key_rows, value_rows, length)
    tensor_count = lax.axis_size("tensor")
    dp_count = lax.axis_size("dp")
    own_cols = o_weight.shape[1]
    narrow = own_cols // tensor_count
    all_heads = lax.all_gather(attended, "tensor", axis=1, tiled=True)
    split_weight = o_weight.reshape(o_weight.shape[0], tensor_count, narrow)
    full_rows = lax.all_to_all(split_weight, "tensor", split_axis=1, concat_axis=0, tiled=True)
    full_rows = full_rows.reshape(full_rows.shape[0], narrow)
    mixed = jnp.dot(
        all_heads,
        lax.all_gather(full_rows, "dp", axis=1, tiled=True),
        preferred_element_type=jnp.float32,
    ).astype(jnp.bfloat16)
    mixed = mixed.reshape(total, tensor_count, dp_count // tensor_count, narrow)
    arrived = lax.all_to_all(mixed, "tensor", split_axis=1, concat_axis=1, tiled=True)
    projected = arrived.transpose(0, 2, 1, 3).reshape(total, -1)
    live = (positions < length)[None, :, None]
    kept_keys = jnp.where(live, key_rows, jnp.zeros_like(key_rows))
    kept_values = jnp.where(live, value_rows, jnp.zeros_like(value_rows))
    cache = jnp.stack([kept_keys, kept_values], axis=0)
    routed = deliver(regroup(cache), destinations)
    return (projected[None], routed[None])


def solution(mesh):
    placed = (
        P(("parts", "dp"), None, None),
        P("dp", "tensor"),
        P("dp", None, "tensor"),
        P("tensor", "dp"),
        P(("parts", "dp")),
        P(("parts", "dp")),
    )
    return jax.shard_map(
        on_device,
        mesh=mesh,
        in_specs=placed,
        out_specs=(
            P(("parts", "dp"), None, "tensor"),
            P(("parts", "dp"), None, None, "tensor", None),
        ),
        check_vma=False,
    )
```

profile of v0, /device:TPU:0, one launch (start us, length us, event | category | flops | bytes accessed | tf_op | source)
XLA Modules:
  0.0 383.2 jit_solution(15370525217813925587)
XLA Ops:
  8.7 1.3 copy.67
  10.0 5.7 %all_to_all.54 = bf16[1024,2,256]{0,2,1:T(8,128)(2,1)S(1)} all-to-all(bf16[1024,2,256]{0,2,1:T(8,128)(2,1)} %bitcast.110), channel_id=1, replica_groups=mesh['parts'=2,'dp'=8,'tensor'=2] {'tensor'}, dimensions={1} | all-to-all | bytes 2097152 | tf_op jit(solution)/shard_map/all_to_all | solution.py:100
  15.7 1.3 copy.68
  18.3 0.8 dynamic-update-slice
  19.1 13.8 %all-reduce = s32[8]{0:T(128)S(1)} all-reduce(s32[8]{0:T(128)S(1)} %dynamic-update-slice), channel_id=1, replica_groups=mesh['parts'=2,'dp'=8,'tensor'=2] {'dp'}, use_global_device_ids=true, to_apply=%add | all-reduce | flops 8 | bytes 64
  34.0 51.9 %all-gather.7.cloned.1.call-done = bf16[4096,2,256]{2,1,0:T(2,128)(2,1)} async-done(((bf16[512,2,256]{2,1,0:T(2,128)(2,1)}), bf16[4096,2,256]{2,1,0:T(2,128)(2,1)}) %all-gather.7.cloned.1.call-update) | async-done | bytes 4194320 | tf_op jit(solution)/shard_map/all_gather | solution.py:78
  85.9 11.3 %copy.80 = bf16[4096,2,256]{0,2,1:T(8,128)(2,1)} copy(bf16[4096,2,256]{2,1,0:T(2,128)(2,1)} %all-gather.7.cloned.1.call-done) | data formatting | bytes 8388608 | tf_op jit(solution)/shard_map/reshape | solution.py:82
  97.2 3.5 fusion.1
  101.7 3.9 %all_to_all.55 = bf16[2,2,256,128]{3,1,0,2:T(2,128)(2,1)S(1)} all-to-all(bf16[2,2,256,128]{3,1,0,2:T(2,128)(2,1)S(1)} %copy.71), channel_id=1, replica_groups=mesh['parts'=2,'dp'=8,'tensor'=2] {'tensor'}, dimensions={2} | all-to-all | bytes 524288 | tf_op jit(solution)/shard_map/all_to_all | solution.py:54
  106.3 2.1 reduce.1
  108.4 0.9 reshape.172
  109.3 3.4 all-to-all-start.3
  112.8 0.7 fusion.12
  113.6 16.2 %all-to-all-done.3 = bf16[8,2,8192]{2,1,0:T(2,128)(2,1)S(1)} async-done(((bf16[8,2,8192]{2,1,0:T(2,128)(2,1)}), bf16[8,2,8192]{2,1,0:T(2,128)(2,1)S(1)}, u32[]{:S(2)}, u32[]{:S(2)}) %all-to-all-start.3) | async-done | bytes 262176 | tf_op jit(solution)/shard_map/all_to_all | solution.py:61
  131.1 85.4 %all-gather.5.cloned.1.call-done = bf16[4096,1024]{1,0:T(8,128)(2,1)} async-done(((bf16[512,1024]{1,0:T(8,128)(2,1)}), bf16[4096,1024]{1,0:T(8,128)(2,1)}) %all-gather.5.cloned.1.call-update) | async-done | bytes 8388624 | tf_op jit(solution)/shard_map/all_gather | solution.py:77
  216.5 11.4 %copy.61 = bf16[1024,4096]{1,0:T(8,128)(2,1)} copy(bf16[1024,4096]{0,1:T(8,128)(2,1)} %bitcast.104) | data formatting | bytes 16777216 | tf_op jit(solution)/shard_map/dot_general | solution.py:80
  228.0 5.8 %fusion.3 = f32[256,8,128]{0,2,1:T(8,128)S(1)} fusion(bf16[8,128,4096]{2,1,0:T(8,128)(2,1)} %bitcast.105, bf16[1,256,4096]{2,1,0:T(8,128)(2,1)S(1)} %copy-done), kind=kOutput, calls=%fused_computation.5 | convolution fusion | flops 2147483648 | bytes 11534336 | tf_op jit(solution)/shard_map/dot_general | solution.py:80
  234.2 1.0 copy.62
  235.3 3.4 fusion.27
  238.6 2.8 convolution_convert_fusion.1
  241.6 0.7 reduce.2
  242.5 16.3 %all_to_all.56 = bf16[8,2,8192]{2,1,0:T(2,128)(2,1)S(1)} all-to-all(bf16[8,2,8192]{2,1,0:T(2,128)(2,1)S(1)} %reshape.174), channel_id=1, replica_groups=mesh['parts'=2,'dp'=8,'tensor'=2] {'dp'}, dimensions={0} | all-to-all | bytes 524288 | tf_op jit(solution)/shard_map/all_to_all | solution.py:66
  259.0 1.6 reduce
  260.6 0.7 copy.84
  261.4 89.1 %all-gather.11.cloned.1.call-done = bf16[2048,2048]{1,0:T(8,128)(2,1)} async-done(((bf16[2048,256]{1,0:T(8,128)(2,1)}), bf16[2048,2048]{1,0:T(8,128)(2,1)}) %all-gather.11.cloned.1.call-update) | async-done | bytes 8388624 | tf_op jit(solution)/shard_map/all_gather | solution.py:104
  350.5 8.6 %all-gather.9.cloned.1.call-done = bf16[256,2048]{0,1:T(8,128)(2,1)} async-done(((bf16[256,1024]{0,1:T(8,128)(2,1)}), bf16[256,2048]{0,1:T(8,128)(2,1)}) %all-gather.9.cloned.1.call-update) | async-done | bytes 1048592 | tf_op jit(solution)/shard_map/all_gather | solution.py:98
  359.1 6.1 %convolution_convert_fusion = bf16[256,2048]{1,0:T(8,128)(2,1)S(1)} fusion(bf16[256,2048]{0,1:T(8,128)(2,1)} %all-gather.9.cloned.1.call-done, bf16[2048,2048]{1,0:T(8,128)(2,1)} %all-gather.11.cloned.1.call-done), kind=kOutput, calls=%fused_computation.2 | convolution fusion | flops 2148007936 | bytes 10485760 | tf_op jit(solution)/shard_map/dot_general | solution.py:102
  365.2 1.6 reshape.153
  366.7 1.6 copy.69
  368.3 4.6 %all_to_all.57 = bf16[256,2,4,256]{3,2,0,1:T(4,128)(2,1)S(1)} all-to-all(bf16[256,2,4,256]{3,2,0,1:T(4,128)(2,1)S(1)} %copy.69), channel_id=1, replica_groups=mesh['parts'=2,'dp'=8,'tensor'=2] {'tensor'}, dimensions={1} | all-to-all | bytes 2097152 | tf_op jit(solution)/shard_map/all_to_all | solution.py:108
  372.9 1.5 copy.70
  374.4 2.3 copy.75
  (42 shorter events, 6.6 us)
Async XLA Ops:
  7.2 90.0 %copy-start = (bf16[1,256,4096]{2,1,0:T(8,128)(2,1)S(1)}, bf16[1,256,4096]{2,1,0:T(8,128)(2,1)}, u32[]{:S(2)}) copy-start(bf16[1,256,4096]{2,1,0:T(8,128)(2,1)} %param.6) | copy-start | bytes 6291460
  7.2 1.5 copy-start.1
  7.2 78.7 %all-gather.7.cloned.1.call-start = ((), (), s32[]{:S(2)}) async-start(), calls=%async_computation.6 | async-start | bytes 4718592 | tf_op jit(solution)/shard_map/all_gather | solution.py:78
  7.9 208.6 %all-gather.5.cloned.1.call-start = ((), (), s32[]{:S(2)}) async-start(), calls=%async_computation.5 | async-start | bytes 9437184 | tf_op jit(solution)/shard_map/all_gather | solution.py:77
  8.7 341.8 %all-gather.11.cloned.1.call-start = ((), (), s32[]{:S(2)}) async-start(), calls=%async_computation.8 | async-start | bytes 9437184 | tf_op jit(solution)/shard_map/all_gather | solution.py:104
  15.7 2.0 copy-start.3
  100.6 0.9 copy-start.2
  109.3 20.5 %all-to-all-start.3 = ((bf16[8,2,8192]{2,1,0:T(2,128)(2,1)}), bf16[8,2,8192]{2,1,0:T(2,128)(2,1)S(1)}, u32[]{:S(2)}, u32[]{:S(2)}) async-start(bf16[8,2,8192]{2,1,0:T(2,128)(2,1)} %reshape.172), calls=%async_computation.3 | async-start | bytes 524288 | tf_op jit(solution)/shard_map/all_to_all | solution.py:61
  112.8 246.3 %all-gather.9.cloned.1.call-start = ((), (), s32[]{:S(2)}) async-start(), calls=%async_computation.7 | async-start | bytes 1572864 | tf_op jit(solution)/shard_map/all_gather | solution.py:98
Sparse Core Ops, SparseCore 0:
  10.1 75.6 all-gather.6
  88.0 128.4 all-gather.4
  219.1 131.2 all-gather.10
  351.9 7.2 all-gather.8
where the time goes:
time: 384 us; the launch traced here: 383 us
  waiting for transfers between devices  253 us (66%)
  blocking collectives  44.3 us (12%)
  local copies, waits for them, and re-layouts  39.8 us (10%)
  matrix products  21.6 us (6%)
  between operations  15.3 us (4%)
  other arithmetic  5.94 us (2%)
    all_gather x1, waiting for transfers between devices, on_device(): lax.all_gather(full_rows, 'dp', axis=1, tiled=True)  89.1 us
    all_gather x1, waiting for transfers between devices, on_device(): lax.all_gather(q_weight, 'dp', axis=0, tiled=True)  85.4 us
    all_gather x1, waiting for transfers between devices, on_device(): lax.all_gather(kv_weight, 'dp', axis=0, tiled=True)  51.9 us
    all_to_all x1, blocking collectives, deliver(): lax.all_to_all(outgoing, 'dp', split_axis=0, concat_axis=0, tiled=True)  16.3 us
    all_to_all x1, waiting for transfers between devices, deliver(): spread = lax.all_to_all(flat, 'dp', split_axis=0, concat_axis=0, tiled=True)  16.2 us
    unnamed x1, blocking collectives  13.8 us
    dot_general x1, local copies, waits for them, and re-layouts, on_device(): query_raw = jnp.dot(tokens, q_full, preferred_element_type=jnp.float32)  11.4 us
    reshape x1, local copies, waits for them, and re-layouts, on_device(): kv_full.reshape(kv_full.shape[0], -1)  11.3 us
  transfers between devices with their start and end apart: 5, of which 5 were waited for; matrix products, arithmetic and copies ran while one was open for 14% of the time, Pallas kernels for 0%

commit v1 on v0

v1 whole, which is shorter than its diff:
```python
import functools
import math

import jax
import jax.numpy as jnp
from jax import lax
from jax.experimental import pallas as pl
from jax.experimental.pallas import tpu as pltpu
from jax.sharding import PartitionSpec as P

HD = 128
ROPE_BASE = 500000.0
MESH = pl.DeviceIdType.MESH
F32 = jnp.float32
BF16 = jnp.bfloat16


def tables(total):
    half = HD // 2
    steps = jnp.arange(half, dtype=F32) * (2.0 / HD)
    freq = jnp.power(jnp.float32(ROPE_BASE), -steps)
    angle = jnp.arange(total, dtype=F32)[:, None] * freq[None, :]
    cosine, sine = jnp.cos(angle), jnp.sin(angle)
    return (
        jnp.concatenate([cosine, cosine], axis=1),
        jnp.concatenate([-sine, sine], axis=1),
    )


def rdma(src, dst, send, recv, **device):
    return pltpu.make_async_remote_copy(
        src_ref=src, dst_ref=dst, send_sem=send, recv_sem=recv,
        device_id=device, device_id_type=MESH,
    )


def kernel(n, groups, group, length_ref, dest_ref, tok, w, o, cos_ref, sin_ref,
           out, cache,
           wbuf, obuf, ptok, acc, psend, precv, asend, arecv, dsend, drecv,
           xsend, xrecv, csend, cflat, spread, going, final, dmine, dall, kbuf,
           wz, wr, wl, wy, wys, oz, orr, ol, oy, oys,
           ts, tr, ps, pr, as_, ar, ds, dr, xs, xr, cs, cr,
           des, der, p1s, p1r, p2s, p2r):
    me = lax.axis_index("dp")
    y = lax.axis_index("parts")
    t = lax.axis_index("tensor")
    z = me // 2
    x = me % 2
    links = n // 2
    mate = z * 2 + (1 - x)
    total = tok.shape[1]
    subs, osubs = w.shape[1], o.shape[1]
    width = group * HD
    block = width + 2 * HD
    half = total // 2
    piece = spread.shape[1]
    homes = links // 2

    barrier = pltpu.get_barrier_semaphore()

    def greet(k, c):
        pl.semaphore_signal(
            barrier, inc=1, device_id={"dp": (me + k) % n}, device_id_type=MESH)
        return c

    lax.fori_loop(1, n, greet, 0)
    pl.semaphore_signal(barrier, inc=1, device_id={"tensor": 1 - t}, device_id_type=MESH)
    pl.semaphore_signal(barrier, inc=1, device_id={"parts": 1 - y}, device_id_type=MESH)
    pl.semaphore_wait(barrier, n + 1)

    class Chain:
        def __init__(self, own, buf, zr, sr, sl, yr, ys, count):
            self.own, self.buf, self.count = own, buf, count
            self.zr, self.sr, self.sl, self.yr, self.ys = zr, sr, sl, yr, ys

        def right(self, a, j, src):
            return rdma(src, self.buf.at[a, y, j], self.sr.at[a, j], self.zr.at[a, j], dp=me + 2)

        def left(self, a, j, src):
            return rdma(src, self.buf.at[a, y, j], self.sl.at[a, j], self.zr.at[a, j], dp=me - 2)

        def across(self, a, j, side):
            part = self.buf.at[a, side, j]
            return rdma(part, part, self.ys.at[a, j], self.yr.at[a, j], parts=1 - y)

        def start_right(self):
            for j in range(self.count):
                self.right(z, j, self.own.at[y, j]).start()

        def start_left(self):
            for j in range(self.count):
                self.left(z, j, self.own.at[y, j]).start()

        def forward(self, s):
            a, b = z - s, z + s
            for j in range(self.count):
                @pl.when(a >= 0)
                def _():
                    src = self.buf.at[a, y, j]
                    self.right(a, j, src).wait_recv()

                    @pl.when(z + 1 < links)
                    def _():
                        self.right(a, j, src).start()
                    self.across(a, j, y).start()

                @pl.when(b < links)
                def _():
                    src = self.buf.at[b, y, j]
                    self.left(b, j, src).wait_recv()

                    @pl.when(z > 0)
                    def _():
                        self.left(b, j, src).start()
                    self.across(b, j, y).start()

        def arrive(self, a):
            for j in range(self.count):
                self.across(a, j, 1 - y).wait_recv()

        def drain(self):
            def one(a, c):
                for j in range(self.count):
                    src = self.buf.at[a, y, j]

                    @pl.when((a <= z) & (z + 1 < links))
                    def _():
                        self.right(a, j, src).wait_send()

                    @pl.when((a >= z) & (z > 0))
                    def _():
                        self.left(a, j, src).wait_send()

                    @pl.when(a != z)
                    def _():
                        self.across(a, j, y).wait_send()
                return c
            lax.fori_loop(0, links, one, 0)

    qkv = Chain(w, wbuf, wz, wr, wl, wy, wys, subs)
    och = Chain(o, obuf, oz, orr, ol, oy, oys, osubs)

    def start_o(s):
        @pl.when((s == z) & (z + 1 < links))
        def _():
            och.start_right()

        @pl.when((s == links - 1 - z) & (z > 0))
        def _():
            och.start_left()

    @pl.when(z + 1 < links)
    def _():
        qkv.start_right()

    @pl.when(z > 0)
    def _():
        qkv.start_left()

    def tokens(a):
        return rdma(tok.at[2 * a + (1 - x)], ptok.at[a], ts.at[a], tr.at[a], dp=mate)

    def send_tokens(k, c):
        tokens((z + k) % links).start()
        return c

    lax.fori_loop(0, links, send_tokens, 0)
    start_o(0)

    slot = jnp.full(dmine.shape, dest_ref[0], jnp.int32)
    dmine[...] = slot
    dall[me] = slot

    def tell(k):
        peer = (me + k) % n
        return rdma(dmine, dall.at[me], des.at[peer], der.at[me], dp=peer)

    def send_slots(k, c):
        tell(k).start()
        return c

    lax.fori_loop(1, n, send_slots, 0)

    wbuf[z] = w[...]
    obuf[z] = o[...]
    acc[...] = jnp.zeros_like(acc)
    depth = tok.shape[2]

    def multiply(a):
        weight = wbuf[a].reshape(depth, wbuf.shape[-1])
        acc[0] += jnp.dot(tok[2 * a + x], weight, preferred_element_type=F32)
        acc[1] += jnp.dot(ptok[a], weight, preferred_element_type=F32)

    def step(s, c):
        qkv.forward(s)
        start_o(s)

        def side(k, c):
            a = jnp.where(k == 0, z - (s - 1), z + (s - 1))

            @pl.when((a >= 0) & (a < links) & ((k == 0) | (s > 1)))
            def _():
                @pl.when(s > 1)
                def _():
                    qkv.arrive(a)
                tokens(a).wait_recv()
                multiply(a)
            return c
        lax.fori_loop(0, 2, side, 0)
        return c

    lax.fori_loop(1, links + 1, step, 0)

    def partial(g):
        return rdma(psend.at[g], precv.at[g], ps.at[g], pr.at[g], dp=mate)

    for g in range(groups):
        psend[g] = acc[1, :, g * block:(g + 1) * block].astype(BF16)
        partial(g).start()

    if links > 1:
        och.forward(1)

    length = length_ref[0]
    cosine, sine = cos_ref[...], sin_ref[...]

    def rotate(u):
        return u * cosine + pltpu.roll(u, HD // 2, axis=1) * sine

    live = lax.broadcasted_iota(jnp.int32, (total, HD), 0) < length
    span = cflat.shape[0] // 2
    run = groups * half

    def regroup(kind):
        rows = pl.ds(pl.multiple_of(kind * span + t * run, half), run)
        return rdma(csend.at[kind], cflat.at[rows], cs.at[kind], cr.at[kind], tensor=1 - t)

    for g in range(groups):
        partial(g).wait_recv()
        lo = g * block + width
        keys = acc[0, :, lo:lo + HD] + precv[g, :, width:width + HD].astype(F32)
        values = acc[0, :, lo + HD:lo + 2 * HD] + precv[g, :, width + HD:].astype(F32)
        for kind, got in enumerate((rotate(keys), values)):
            kbuf[kind, g] = got.astype(BF16)
            kept = jnp.where(live, got, 0.0)
            first, second = kept[:half], kept[half:]
            mine = jnp.where(t == 0, first, second).astype(BF16)
            other = jnp.where(t == 0, second, first).astype(BF16)
            csend[kind, g * half:(g + 1) * half] = other
            start = pl.multiple_of(kind * span + t * run + g * half, half)
            cflat[pl.ds(start, half)] = mine
    for kind in range(2):
        regroup(kind).start()

    def rows_of(p):
        return pl.ds(pl.multiple_of(p * piece, piece), piece)

    def spread_to(k):
        peer = (me + k) % n
        return rdma(cflat.at[rows_of(peer)], spread.at[me], p1s.at[peer], p1r.at[me], dp=peer)

    for kind in range(2):
        other = pl.ds(pl.multiple_of(kind * span + (1 - t) * run, half), run)
        rdma(csend.at[kind], cflat.at[other], cs.at[kind], cr.at[kind], tensor=1 - t).wait_recv()

    def send_spread(k, c):
        spread_to(k).start()
        return c

    lax.fori_loop(1, n, send_spread, 0)
    spread[me] = cflat[rows_of(me)]

    row = lax.broadcasted_iota(jnp.int32, (total, total), 0)
    col = lax.broadcasted_iota(jnp.int32, (total, total), 1)
    allowed = (row >= col) & (col < length)

    def attended(g):
        return rdma(asend.at[g], arecv.at[g], as_.at[g], ar.at[g], dp=mate)

    for g in range(groups):
        keys, values = kbuf[0, g], kbuf[1, g]
        for h in range(group):
            lo = g * block + h * HD
            raw = acc[0, :, lo:lo + HD] + precv[g, :, h * HD:(h + 1) * HD].astype(F32)
            query = rotate(raw).astype(BF16)
            scores = lax.dot_general(
                query, keys, (((1,), (1,)), ((), ())), preferred_element_type=F32
            ) / math.sqrt(HD)
            scores = jnp.where(allowed, scores, -jnp.inf)
            peak = jnp.max(scores, axis=-1, keepdims=True)
            expo = jnp.exp(scores - peak)
            weights = (expo / jnp.sum(expo, axis=-1, keepdims=True)).astype(BF16)
            asend[g, :, h * HD:(h + 1) * HD] = jnp.dot(
                weights, values, preferred_element_type=F32).astype(BF16)
        attended(g).start()

    def rest(s, c):
        och.forward(s)
        return c

    lax.fori_loop(2, links, rest, 0)

    def wait_first(k, c):
        p = (me + k) % n
        rdma(dmine, dall.at[p], des.at[p], der.at[p], dp=p).wait_recv()
        rdma(cflat.at[rows_of(p)], spread.at[p], p1s.at[p], p1r.at[p], dp=p).wait_recv()
        return c

    lax.fori_loop(1, n, wait_first, 0)

    def hand(s):
        return rdma(going.at[s], final.at[me], p2s.at[s], p2r.at[me], dp=s)

    def route(k, c):
        s = (me + k) % n

        def add(p, value):
            mask = (dall[p][0:1, :] == s).astype(F32)
            return value + spread[p].astype(F32) * mask

        got = lax.fori_loop(0, n, add, jnp.zeros((piece, HD), F32)).astype(BF16)

        @pl.when(k > 0)
        def _():
            going[s] = got
            hand(s).start()

        @pl.when(k == 0)
        def _():
            final[me] = got
        return c

    lax.fori_loop(0, n, route, 0)

    def await_o(a, c):
        @pl.when(a != z)
        def _():
            och.arrive(a)
        return c

    lax.fori_loop(0, links, await_o, 0)
    for g in range(groups):
        attended(g).wait_recv()

    def project(a, ref):
        value = None
        for g in range(groups):
            weight = obuf[a].reshape(groups, width, obuf.shape[-1])[g]
            term = jnp.dot(ref[g], weight, preferred_element_type=F32)
            value = term if value is None else value + term
        return value

    def swap(i):
        return rdma(dsend.at[i], drecv.at[i], ds.at[i], dr.at[i], tensor=1 - t)

    def away(i, c):
        a = (1 - t) * homes + i
        dsend[i, 1] = project(a, arecv)
        dsend[i, 0] = project(a, asend)
        swap(i).start()
        return c

    lax.fori_loop(0, homes, away, 0)

    def give(i):
        return rdma(xsend.at[i], xrecv.at[i], xs.at[i], xr.at[i], dp=mate)

    def home(i, c):
        a = t * homes + i
        theirs, ours = project(a, arecv), project(a, asend)
        swap(i).wait_recv()
        xsend[i] = (theirs + drecv[i, 1]).astype(BF16)
        give(i).start()
        out[2 * i + x] = (ours + drecv[i, 0]).astype(BF16)
        return c

    lax.fori_loop(0, homes, home, 0)

    def last(k, c):
        p = (me + k) % n
        rdma(going.at[p], final.at[p], p2s.at[p], p2r.at[p], dp=p).wait_recv()
        return c

    lax.fori_loop(1, n, last, 0)
    cache[...] = final[...]

    def take(i, c):
        give(i).wait_recv()
        out[2 * i + (1 - x)] = xrecv[i]
        return c

    lax.fori_loop(0, homes, take, 0)

    qkv.drain()
    och.drain()

    def drain_tokens(a, c):
        tokens(a).wait_send()
        return c

    lax.fori_loop(0, links, drain_tokens, 0)
    for g in range(groups):
        partial(g).wait_send()
        attended(g).wait_send()
    for kind in range(2):
        regroup(kind).wait_send()

    def drain_peers(k, c):
        tell(k).wait_send()
        spread_to(k).wait_send()
        hand((me + k) % n).wait_send()
        return c

    lax.fori_loop(1, n, drain_peers, 0)

    def drain_homes(i, c):
        swap(i).wait_send()
        give(i).wait_send()
        return c

    lax.fori_loop(0, homes, drain_homes, 0)


def pieces_of(rows, columns):
    count = 2
    if rows % 32 or rows * columns * 2 < 262144:
        count = 1
    return count


def on_device(n, normed, q_weight, kv_weight, o_weight, lengths, destinations):
    total, model = normed.shape[1], normed.shape[2]
    rows, q_columns = q_weight.shape
    groups = kv_weight.shape[2] // HD
    group = q_columns // HD // groups
    width = group * HD
    parts = []
    for g in range(groups):
        parts.append(q_weight[:, g * width:(g + 1) * width])
        parts.append(kv_weight[:, 0, g * HD:(g + 1) * HD])
        parts.append(kv_weight[:, 1, g * HD:(g + 1) * HD])
    w = jnp.concatenate(parts, axis=1)
    columns = w.shape[1]
    subs = pieces_of(rows // 2, columns)
    w = w.reshape(2, subs, rows // 2 // subs, columns)
    o_rows, o_columns = o_weight.shape
    osubs = pieces_of(o_rows // 2, o_columns)
    o = o_weight.reshape(2, osubs, o_rows // 2 // osubs, o_columns)
    tok = normed[0].reshape(total, n, rows).transpose(1, 0, 2)
    cosine, sine = tables(total)
    links, homes = n // 2, n // 4
    block = width + 2 * HD
    half = total // 2
    cache_rows = 2 * 2 * groups * half
    piece = cache_rows // n
    dma = pltpu.SemaphoreType.DMA
    vmem = pltpu.VMEM
    space = pl.BlockSpec(memory_space=pltpu.VMEM)
    smem = pl.BlockSpec(memory_space=pltpu.SMEM)
    chain = lambda count: [dma((links, count))] * 5
    out, cache = pl.pallas_call(
        functools.partial(kernel, n, groups, group),
        out_shape=(
            jax.ShapeDtypeStruct((n // 2, total, o_columns), BF16),
            jax.ShapeDtypeStruct((n, piece, HD), BF16),
        ),
        in_specs=[smem, smem] + [space] * 5,
        out_specs=(space, space),
        scratch_shapes=[
            vmem((links,) + w.shape, BF16),
            vmem((links,) + o.shape, BF16),
            vmem((links, total, rows), BF16),
            vmem((2, total, columns), F32),
            vmem((groups, total, block), BF16),
            vmem((groups, total, block), BF16),
            vmem((groups, total, width), BF16),
            vmem((groups, total, width), BF16),
            vmem((homes, 2, total, o_columns), F32),
            vmem((homes, 2, total, o_columns), F32),
            vmem((homes, total, o_columns), BF16),
            vmem((homes, total, o_columns), BF16),
            vmem((2, groups * half, HD), BF16),
            vmem((cache_rows, HD), BF16),
            vmem((n, piece, HD), BF16),
            vmem((n, piece, HD), BF16),
            vmem((n, piece, HD), BF16),
            vmem((8, HD), jnp.int32),
            vmem((n, 8, HD), jnp.int32),
            vmem((2, groups, total, HD), BF16),
        ]
        + chain(subs) + chain(osubs)
        + [dma((links,))] * 2 + [dma((groups,))] * 4 + [dma((homes,))] * 4
        + [dma((2,))] * 2 + [dma((n,))] * 6,
        compiler_params=pltpu.CompilerParams(
            collective_id=0, has_side_effects=True, vmem_limit_bytes=60 * 1024 * 1024
        ),
    )(lengths, destinations, tok, w, o, cosine, sine)
    projected = out.transpose(1, 0, 2).reshape(1, total, -1)
    return projected, cache.reshape(1, 2, 2 * groups, half, HD)


def solution(mesh):
    placed = (
        P(("parts", "dp"), None, None),
        P("dp", "tensor"),
        P("dp", None, "tensor"),
        P("tensor", "dp"),
        P(("parts", "dp")),
        P(("parts", "dp")),
    )
    return jax.shard_map(
        functools.partial(on_device, mesh.shape["dp"]),
        mesh=mesh,
        in_specs=placed,
        out_specs=(
            P(("parts", "dp"), None, "tensor"),
            P(("parts", "dp"), None, None, "tensor", None),
        ),
        check_vma=False,
    )
```

time: 384 us -> 149 us (0.39)
  waiting for transfers between devices: 253 us -> 0 us
  Pallas kernels: 0 us -> 134 us
  blocking collectives: 44.3 us -> 0 us
  local copies, waits for them, and re-layouts: 39.8 us -> 11.9 us
  matrix products: 21.6 us -> 0 us
  between operations: 15.3 us -> 2.08 us
  other arithmetic: 5.94 us -> 1.36 us
    all_gather x4 -> x0, waiting for transfers between devices: 235 us -> none  [the longest x1 89.1 us: on_device(): lax.all_gather(full_rows, 'dp', axis=1, tiled=True)]
    pallas_call x0 -> x1, Pallas kernels: none -> 134 us  [on_device(): pl.pallas_call(functools.partial(kernel, n, groups, group), out_shape=(ja...]
    all_to_all x4 -> x0, blocking collectives: 30.5 us -> none  [the longest x1 16.3 us: deliver(): lax.all_to_all(outgoing, 'dp', split_axis=0, concat_axis=0, tiled=True)]
    dot_general x4 -> x0, matrix products: 18.2 us -> none  [the longest x1 6.06 us: on_device(): jnp.dot(all_heads, lax.all_gather(full_rows, 'dp', axis=1, tiled=True), p...]
    all_to_all x1 -> x0, waiting for transfers between devices: 16.2 us -> none  [deliver(): spread = lax.all_to_all(flat, 'dp', split_axis=0, concat_axis=0, tiled=True)]
    reshape x3 -> x0, local copies, waits for them, and re-layouts: 14.5 us -> none  [the longest x1 11.3 us: on_device(): kv_full.reshape(kv_full.shape[0], -1)]
    unnamed x1 -> x0, blocking collectives: 13.8 us -> none
    dot_general x1 -> x0, local copies, waits for them, and re-layouts: 11.4 us -> none  [on_device(): query_raw = jnp.dot(tokens, q_full, preferred_element_type=jnp.float32)]
  transfers between devices with their start and end apart: 5 -> 0, of which waited for: 5 -> 0; matrix products, arithmetic and copies ran while one was open for 14% -> 0% of each run, Pallas kernels for 0% -> 0%
where the time goes in v1:
time: 149 us
  Pallas kernels  134 us (90%)
  local copies, waits for them, and re-layouts  11.9 us (8%)
  between operations  2.08 us (1%)
    pallas_call x1, Pallas kernels, on_device(): pl.pallas_call(functools.partial(kernel, n, groups, group), out_shape=(ja...  134 us
    unnamed x18, local copies, waits for them, and re-layouts  5.66 us

profile of v1, /device:TPU:0, one launch (start us, length us, event | category | flops | bytes accessed | tf_op | source)
XLA Modules:
  0.0 148.9 jit_solution(2635343269972608652)
XLA Ops:
  0.6 0.0 copy-start.1
  0.6 2.2 %fusion.4 = (bf16[512,1,128]{2,1,0:T(2,128)(2,1)S(1)}, bf16[512,1,128]{2,1,0:T(2,128)(2,1)S(1)}, bf16[512,1,128]{2,1,0:T(2,128)(2,1)S(1)}, bf16[512,1,128]{2,1,0:T(2,128)(2,1)S(1)}) fusion(bf16[512,2,256]{2,1,0:T(2,128)(2,1)} %param.8), kind=kLoop, calls=%fused_computation.14 | loop fusion | bytes 1048576 | tf_op jit(solution)/shard_map/slice | solution.py:441
  2.9 0.0 copy-done.1
  2.9 0.1 fusion.3
  3.3 0.0 copy-start
  3.3 0.5 fusion.2
  3.9 0.8 pad_maximum_fusion
  4.7 0.0 copy-done
  4.7 3.3 %copy.8 = bf16[1,256,4096]{1,2,0:T(8,128)(2,1)S(1)} copy(bf16[1,256,4096]{2,1,0:T(8,128)(2,1)} %param.6) | data formatting | bytes 4194304 | tf_op args[0]
  8.0 2.4 %copy.9 = bf16[256,8,512]{2,0,1:T(8,128)(2,1)} copy(bf16[256,8,512]{0,2,1:T(8,128)(2,1)S(1)} %bitcast.13) | data formatting | bytes 4194304 | tf_op jit(solution)/shard_map/reshape;squeeze | solution.py:449
  11.7 133.6 %shard_map.77 = (bf16[4,256,512]{2,1,0:T(8,128)(2,1)}, bf16[8,128,128]{2,1,0:T(8,128)(2,1)}) custom-call(s32[1]{0:T(128)S(6)} %copy.26.length_ref, s32[1]{0:T(128)S(6)} %copy.27.dest_ref, bf16[8,256,512]{2,1,0:T(8,128)(2,1)} %bitcast.12, bf16[2,2,128,1536]{3,2,1,0:T(8,128)(2,1)} %copy-done, bf16[2,2,256,512]{3,2,1,0:T(8,128)(2,1)} %bitcast.18, ...), custom_call_target="tpu_custom_call" | custom-call | tf_op jit(solution)/shard_map/pallas_call | solution.py:461
  145.3 1.5 copy.14
  146.8 0.0 copy-start.2
  146.8 1.4 copy.15
  148.2 0.0 copy-done.2
  148.2 0.7 copy.28
  (11 shorter events, 0.3 us)
Async XLA Ops:
  0.6 2.3 %copy-start.1 = (bf16[512,1024]{1,0:T(8,128)(2,1)S(1)}, bf16[512,1024]{1,0:T(8,128)(2,1)}, u32[]{:S(2)}) copy-start(bf16[512,1024]{1,0:T(8,128)(2,1)} %param.7) | copy-start | bytes 3145732
  3.3 1.4 copy-start
  146.8 1.4 copy-start.2

commit v2 on v1

--- a/solution.py
+++ b/solution.py
@@ -34,7 +34,7 @@
     )
 
 
-def kernel(n, groups, group, length_ref, dest_ref, tok, w, o, cos_ref, sin_ref,
+def kernel(n, groups, group, length_ref, dest_ref, tok, q, kv, o, cos_ref, sin_ref,
            out, cache,
            wbuf, obuf, ptok, acc, psend, precv, asend, arecv, dsend, drecv,
            xsend, xrecv, csend, cflat, spread, going, final, dmine, dall, kbuf,
@@ -48,13 +48,20 @@
     x = me % 2
     links = n // 2
     mate = z * 2 + (1 - x)
-    total = tok.shape[1]
-    subs, osubs = w.shape[1], o.shape[1]
+    total = cos_ref.shape[0]
+    depth, ocols = q.shape[0], o.shape[-1]
+    subs, osubs = wbuf.shape[3], o.shape[1]
+    flat = depth % HD == 0
     width = group * HD
     block = width + 2 * HD
     half = total // 2
     piece = spread.shape[1]
     homes = links // 2
+
+    for g in range(groups):
+        shape = wbuf.shape[2:5]
+        wbuf[g, z, :, :, :, :width] = q[:, g * width:(g + 1) * width].reshape(shape + (width,))
+        wbuf[g, z, :, :, :, width:] = kv[g].reshape(shape + (2 * HD,))
 
     barrier = pltpu.get_barrier_semaphore()
 
@@ -137,36 +144,44 @@
                 return c
             lax.fori_loop(0, links, one, 0)
 
-    qkv = Chain(w, wbuf, wz, wr, wl, wy, wys, subs)
+    chains = [
+        Chain(wbuf.at[g, z], wbuf.at[g], *(sem.at[g] for sem in (wz, wr, wl, wy, wys)), subs)
+        for g in range(groups)
+    ]
     och = Chain(o, obuf, oz, orr, ol, oy, oys, osubs)
 
-    def start_o(s):
+    chains.append(och)
+
+    def follow(g, s):
         @pl.when((s == z) & (z + 1 < links))
         def _():
-            och.start_right()
+            chains[g + 1].start_right()
 
         @pl.when((s == links - 1 - z) & (z > 0))
         def _():
-            och.start_left()
+            chains[g + 1].start_left()
 
     @pl.when(z + 1 < links)
     def _():
-        qkv.start_right()
+        chains[0].start_right()
 
     @pl.when(z > 0)
     def _():
-        qkv.start_left()
+        chains[0].start_left()
+
+    def columns_of(d):
+        if flat:
+            return tok.at[:, pl.ds(pl.multiple_of(d * depth, HD), depth)]
+        return tok.at[d]
 
     def tokens(a):
-        return rdma(tok.at[2 * a + (1 - x)], ptok.at[a], ts.at[a], tr.at[a], dp=mate)
+        return rdma(columns_of(2 * a + (1 - x)), ptok.at[a], ts.at[a], tr.at[a], dp=mate)
 
     def send_tokens(k, c):
         tokens((z + k) % links).start()
         return c
 
     lax.fori_loop(0, links, send_tokens, 0)
-    start_o(0)
-
     slot = jnp.full(dmine.shape, dest_ref[0], jnp.int32)
     dmine[...] = slot
     dall[me] = slot
@@ -181,41 +196,41 @@
 
     lax.fori_loop(1, n, send_slots, 0)
 
-    wbuf[z] = w[...]
     obuf[z] = o[...]
     acc[...] = jnp.zeros_like(acc)
-    depth = tok.shape[2]
-
-    def multiply(a):
-        weight = wbuf[a].reshape(depth, wbuf.shape[-1])
-        acc[0] += jnp.dot(tok[2 * a + x], weight, preferred_element_type=F32)
-        acc[1] += jnp.dot(ptok[a], weight, preferred_element_type=F32)
-
-    def step(s, c):
-        qkv.forward(s)
-        start_o(s)
-
-        def side(k, c):
-            a = jnp.where(k == 0, z - (s - 1), z + (s - 1))
-
-            @pl.when((a >= 0) & (a < links) & ((k == 0) | (s > 1)))
-            def _():
-                @pl.when(s > 1)
-                def _():
-                    qkv.arrive(a)
-                tokens(a).wait_recv()
-                multiply(a)
-            return c
-        lax.fori_loop(0, 2, side, 0)
-        return c
-
-    lax.fori_loop(1, links + 1, step, 0)
+
+    def multiply(g, a):
+        weight = wbuf[g, a].reshape(depth, block)
+        acc[g, 0] += jnp.dot(columns_of(2 * a + x)[...], weight, preferred_element_type=F32)
+        acc[g, 1] += jnp.dot(ptok[a], weight, preferred_element_type=F32)
 
     def partial(g):
         return rdma(psend.at[g], precv.at[g], ps.at[g], pr.at[g], dp=mate)
 
     for g in range(groups):
-        psend[g] = acc[1, :, g * block:(g + 1) * block].astype(BF16)
+        follow(g, 0)
+
+        def step(s, c, g=g):
+            chains[g].forward(s)
+            follow(g, s)
+
+            def side(k, c):
+                a = jnp.where(k == 0, z - (s - 1), z + (s - 1))
+
+                @pl.when((a >= 0) & (a < links) & ((k == 0) | (s > 1)))
+                def _():
+                    @pl.when(s > 1)
+                    def _():
+                        chains[g].arrive(a)
+                    if g == 0:
+                        tokens(a).wait_recv()
+                    multiply(g, a)
+                return c
+            lax.fori_loop(0, 2, side, 0)
+            return c
+
+        lax.fori_loop(1, links + 1, step, 0)
+        psend[g] = acc[g, 1].astype(BF16)
         partial(g).start()
 
     if links > 1:
@@ -235,11 +250,17 @@
         rows = pl.ds(pl.multiple_of(kind * span + t * run, half), run)
         return rdma(csend.at[kind], cflat.at[rows], cs.at[kind], cr.at[kind], tensor=1 - t)
 
+    row = lax.broadcasted_iota(jnp.int32, (total, total), 0)
+    col = lax.broadcasted_iota(jnp.int32, (total, total), 1)
+    allowed = (row >= col) & (col < length)
+
+    def attended(g):
+        return rdma(asend.at[g], arecv.at[g], as_.at[g], ar.at[g], dp=mate)
+
     for g in range(groups):
         partial(g).wait_recv()
-        lo = g * block + width
-        keys = acc[0, :, lo:lo + HD] + precv[g, :, width:width + HD].astype(F32)
-        values = acc[0, :, lo + HD:lo + 2 * HD] + precv[g, :, width + HD:].astype(F32)
+        keys = acc[g, 0, :, width:width + HD] + precv[g, :, width:width + HD].astype(F32)
+        values = acc[g, 0, :, width + HD:] + precv[g, :, width + HD:].astype(F32)
         for kind, got in enumerate((rotate(keys), values)):
             kbuf[kind, g] = got.astype(BF16)
             kept = jnp.where(live, got, 0.0)
@@ -249,39 +270,13 @@
             csend[kind, g * half:(g + 1) * half] = other
             start = pl.multiple_of(kind * span + t * run + g * half, half)
             cflat[pl.ds(start, half)] = mine
-    for kind in range(2):
-        regroup(kind).start()
-
-    def rows_of(p):
-        return pl.ds(pl.multiple_of(p * piece, piece), piece)
-
-    def spread_to(k):
-        peer = (me + k) % n
-        return rdma(cflat.at[rows_of(peer)], spread.at[me], p1s.at[peer], p1r.at[me], dp=peer)
-
-    for kind in range(2):
-        other = pl.ds(pl.multiple_of(kind * span + (1 - t) * run, half), run)
-        rdma(csend.at[kind], cflat.at[other], cs.at[kind], cr.at[kind], tensor=1 - t).wait_recv()
-
-    def send_spread(k, c):
-        spread_to(k).start()
-        return c
-
-    lax.fori_loop(1, n, send_spread, 0)
-    spread[me] = cflat[rows_of(me)]
-
-    row = lax.broadcasted_iota(jnp.int32, (total, total), 0)
-    col = lax.broadcasted_iota(jnp.int32, (total, total), 1)
-    allowed = (row >= col) & (col < length)
-
-    def attended(g):
-        return rdma(asend.at[g], arecv.at[g], as_.at[g], ar.at[g], dp=mate)
-
-    for g in range(groups):
+        if g == groups - 1:
+            for kind in range(2):
+                regroup(kind).start()
         keys, values = kbuf[0, g], kbuf[1, g]
         for h in range(group):
-            lo = g * block + h * HD
-            raw = acc[0, :, lo:lo + HD] + precv[g, :, h * HD:(h + 1) * HD].astype(F32)
+            lo = h * HD
+            raw = acc[g, 0, :, lo:lo + HD] + precv[g, :, lo:lo + HD].astype(F32)
             query = rotate(raw).astype(BF16)
             scores = lax.dot_general(
                 query, keys, (((1,), (1,)), ((), ())), preferred_element_type=F32
@@ -290,15 +285,76 @@
             peak = jnp.max(scores, axis=-1, keepdims=True)
             expo = jnp.exp(scores - peak)
             weights = (expo / jnp.sum(expo, axis=-1, keepdims=True)).astype(BF16)
-            asend[g, :, h * HD:(h + 1) * HD] = jnp.dot(
+            asend[g, :, lo:lo + HD] = jnp.dot(
                 weights, values, preferred_element_type=F32).astype(BF16)
         attended(g).start()
 
+    def rows_of(p):
+        return pl.ds(pl.multiple_of(p * piece, piece), piece)
+
+    def spread_to(k):
+        peer = (me + k) % n
+        return rdma(cflat.at[rows_of(peer)], spread.at[me], p1s.at[peer], p1r.at[me], dp=peer)
+
+    for kind in range(2):
+        other = pl.ds(pl.multiple_of(kind * span + (1 - t) * run, half), run)
+        rdma(csend.at[kind], cflat.at[other], cs.at[kind], cr.at[kind], tensor=1 - t).wait_recv()
+
+    def send_spread(k, c):
+        spread_to(k).start()
+        return c
+
+    lax.fori_loop(1, n, send_spread, 0)
+    spread[me] = cflat[rows_of(me)]
+
     def rest(s, c):
         och.forward(s)
         return c
 
     lax.fori_loop(2, links, rest, 0)
+
+    def await_o(a, c):
+        @pl.when(a != z)
+        def _():
+            och.arrive(a)
+        return c
+
+    lax.fori_loop(0, links, await_o, 0)
+    def project(a, ref):
+        value = None
+        for g in range(groups):
+            weight = obuf[a].reshape(groups, width, ocols)[g]
+            term = jnp.dot(ref[g], weight, preferred_element_type=F32)
+            value = term if value is None else value + term
+        return value
+
+    def swap(i, side):
+        return rdma(dsend.at[i, side], drecv.at[i, side], ds.at[i, side], dr.at[i, side],
+                    tensor=1 - t)
+
+    def away(side, ref):
+        def one(i, c):
+            dsend[i, side] = project((1 - t) * homes + i, ref)
+            swap(i, side).start()
+            return c
+        lax.fori_loop(0, homes, one, 0)
+
+    away(0, asend)
+    for g in range(groups):
+        attended(g).wait_recv()
+    away(1, arecv)
+
+    def give(i):
+        return rdma(xsend.at[i], xrecv.at[i], xs.at[i], xr.at[i], dp=mate)
+
+    def theirs(i, c):
+        value = project(t * homes + i, arecv)
+        swap(i, 1).wait_recv()
+        xsend[i] = (value + drecv[i, 1]).astype(BF16)
+        give(i).start()
+        return c
+
+    lax.fori_loop(0, homes, theirs, 0)
 
     def wait_first(k, c):
         p = (me + k) % n
@@ -332,49 +388,19 @@
 
     lax.fori_loop(0, n, route, 0)
 
-    def await_o(a, c):
-        @pl.when(a != z)
-        def _():
-            och.arrive(a)
-        return c
-
-    lax.fori_loop(0, links, await_o, 0)
-    for g in range(groups):
-        attended(g).wait_recv()
-
-    def project(a, ref):
-        value = None
-        for g in range(groups):
-            weight = obuf[a].reshape(groups, width, obuf.shape[-1])[g]
-            term = jnp.dot(ref[g], weight, preferred_element_type=F32)
-            value = term if value is None else value + term
-        return value
-
-    def swap(i):
-        return rdma(dsend.at[i], drecv.at[i], ds.at[i], dr.at[i], tensor=1 - t)
-
-    def away(i, c):
-        a = (1 - t) * homes + i
-        dsend[i, 1] = project(a, arecv)
-        dsend[i, 0] = project(a, asend)
-        swap(i).start()
-        return c
-
-    lax.fori_loop(0, homes, away, 0)
-
-    def give(i):
-        return rdma(xsend.at[i], xrecv.at[i], xs.at[i], xr.at[i], dp=mate)
-
-    def home(i, c):
-        a = t * homes + i
-        theirs, ours = project(a, arecv), project(a, asend)
-        swap(i).wait_recv()
-        xsend[i] = (theirs + drecv[i, 1]).astype(BF16)
-        give(i).start()
-        out[2 * i + x] = (ours + drecv[i, 0]).astype(BF16)
-        return c
-
-    lax.fori_loop(0, homes, home, 0)
+    def put(d, value):
+        if ocols % HD == 0:
+            out[:, pl.ds(pl.multiple_of(d * ocols, HD), ocols)] = value
+        else:
+            out[d] = value
+
+    def ours(i, c):
+        value = project(t * homes + i, asend)
+        swap(i, 0).wait_recv()
+        put(2 * i + x, (value + drecv[i, 0]).astype(BF16))
+        return c
+
+    lax.fori_loop(0, homes, ours, 0)
 
     def last(k, c):
         p = (me + k) % n
@@ -386,13 +412,13 @@
 
     def take(i, c):
         give(i).wait_recv()
-        out[2 * i + (1 - x)] = xrecv[i]
+        put(2 * i + (1 - x), xrecv[i])
         return c
 
     lax.fori_loop(0, homes, take, 0)
 
-    qkv.drain()
-    och.drain()
+    for one in chains:
+        one.drain()
 
     def drain_tokens(a, c):
         tokens(a).wait_send()
@@ -414,7 +440,8 @@
     lax.fori_loop(1, n, drain_peers, 0)
 
     def drain_homes(i, c):
-        swap(i).wait_send()
+        swap(i, 0).wait_send()
+        swap(i, 1).wait_send()
         give(i).wait_send()
         return c
 
@@ -434,22 +461,19 @@
     groups = kv_weight.shape[2] // HD
     group = q_columns // HD // groups
     width = group * HD
-    parts = []
-    for g in range(groups):
-        parts.append(q_weight[:, g * width:(g + 1) * width])
-        parts.append(kv_weight[:, 0, g * HD:(g + 1) * HD])
-        parts.append(kv_weight[:, 1, g * HD:(g + 1) * HD])
-    w = jnp.concatenate(parts, axis=1)
-    columns = w.shape[1]
-    subs = pieces_of(rows // 2, columns)
-    w = w.reshape(2, subs, rows // 2 // subs, columns)
+    block = width + 2 * HD
+    kv = kv_weight.reshape(rows, 2, groups, HD).transpose(2, 0, 1, 3)
+    kv = kv.reshape(groups, rows, 2 * HD)
+    subs = pieces_of(rows // 2, block)
+    shard = (2, subs, rows // 2 // subs, block)
     o_rows, o_columns = o_weight.shape
     osubs = pieces_of(o_rows // 2, o_columns)
     o = o_weight.reshape(2, osubs, o_rows // 2 // osubs, o_columns)
-    tok = normed[0].reshape(total, n, rows).transpose(1, 0, 2)
+    tok = normed[0]
+    if rows % HD:
+        tok = tok.reshape(total, n, rows).transpose(1, 0, 2)
     cosine, sine = tables(total)
     links, homes = n // 2, n // 4
-    block = width + 2 * HD
     half = total // 2
     cache_rows = 2 * 2 * groups * half
     piece = cache_rows // n
@@ -457,20 +481,23 @@
     vmem = pltpu.VMEM
     space = pl.BlockSpec(memory_space=pltpu.VMEM)
     smem = pl.BlockSpec(memory_space=pltpu.SMEM)
-    chain = lambda count: [dma((links, count))] * 5
+    straight = o_columns % HD == 0
+    shape = (n // 2, total, o_columns)
+    if straight:
+        shape = (total, n // 2 * o_columns)
     out, cache = pl.pallas_call(
         functools.partial(kernel, n, groups, group),
         out_shape=(
-            jax.ShapeDtypeStruct((n // 2, total, o_columns), BF16),
+            jax.ShapeDtypeStruct(shape, BF16),
             jax.ShapeDtypeStruct((n, piece, HD), BF16),
         ),
-        in_specs=[smem, smem] + [space] * 5,
+        in_specs=[smem, smem] + [space] * 6,
         out_specs=(space, space),
         scratch_shapes=[
-            vmem((links,) + w.shape, BF16),
+            vmem((groups, links) + shard, BF16),
             vmem((links,) + o.shape, BF16),
             vmem((links, total, rows), BF16),
-            vmem((2, total, columns), F32),
+            vmem((groups, 2, total, block), F32),
             vmem((groups, total, block), BF16),
             vmem((groups, total, block), BF16),
             vmem((groups, total, width), BF16),
@@ -488,14 +515,16 @@
             vmem((n, 8, HD), jnp.int32),
             vmem((2, groups, total, HD), BF16),
         ]
-        + chain(subs) + chain(osubs)
-        + [dma((links,))] * 2 + [dma((groups,))] * 4 + [dma((homes,))] * 4
+        + [dma((groups, links, subs))] * 5 + [dma((links, osubs))] * 5
+        + [dma((links,))] * 2 + [dma((groups,))] * 4 + [dma((homes, 2))] * 2 + [dma((homes,))] * 2
         + [dma((2,))] * 2 + [dma((n,))] * 6,
         compiler_params=pltpu.CompilerParams(
             collective_id=0, has_side_effects=True, vmem_limit_bytes=60 * 1024 * 1024
         ),
-    )(lengths, destinations, tok, w, o, cosine, sine)
-    projected = out.transpose(1, 0, 2).reshape(1, total, -1)
+    )(lengths, destinations, tok, q_weight, kv, o, cosine, sine)
+    if not straight:
+        out = out.transpose(1, 0, 2)
+    projected = out.reshape(1, total, -1)
     return projected, cache.reshape(1, 2, 2 * groups, half, HD)
 
 

time: 149 us -> 133 us (0.89)
  Pallas kernels: 134 us -> 125 us
  local copies, waits for them, and re-layouts: 11.9 us -> 4.55 us
    pallas_call x1, Pallas kernels: 134 us -> 125 us  [on_device(): pl.pallas_call(functools.partial(kernel, n, groups, group), out_shape=(ja...]
    unnamed x18 -> x6, local copies, waits for them, and re-layouts: 5.66 us -> 3.06 us
    another operation x1 -> x0, local copies, waits for them, and re-layouts: 2.4 us -> none  [on_device(): tok = normed[0].reshape(total, n, rows).transpose(1, 0, 2)]
    slice x2 -> x0, local copies, waits for them, and re-layouts: 2.3 us -> none  [the longest x1 2.22 us: on_device(): parts.append(kv_weight[:, 1, g * HD:(g + 1) * HD])]
where the time goes in v2:
time: 133 us
  Pallas kernels  125 us (94%)
  local copies, waits for them, and re-layouts  4.55 us (3%)
  between operations  2.02 us (2%)
  other arithmetic  1.35 us (1%)
    pallas_call x1, Pallas kernels, on_device(): pl.pallas_call(functools.partial(kernel, n, groups, group), out_shape=(ja...  125 us
    unnamed x6, local copies, waits for them, and re-layouts  3.06 us

profile of v2, /device:TPU:0, one launch (start us, length us, event | category | flops | bytes accessed | tf_op | source)
XLA Modules:
  0.0 132.7 jit_solution(15054630648392153653)
XLA Ops:
  0.6 0.0 copy-start
  2.0 0.5 fusion.2
  2.5 0.8 pad_maximum_fusion
  3.4 0.0 copy-done
  3.4 0.4 bitcast_bitcast_fusion
  3.7 1.1 reshape.26.kv
  4.9 124.8 %shard_map.77 = (bf16[256,2048]{1,0:T(8,128)(2,1)}, bf16[8,128,128]{2,1,0:T(8,128)(2,1)}) custom-call(s32[1]{0:T(128)S(6)} %copy.13.length_ref, s32[1]{0:T(128)S(6)} %copy.14.dest_ref, bf16[256,4096]{1,0:T(8,128)(2,1)} %bitcast.11, bf16[512,1024]{1,0:T(8,128)(2,1)} %q.1, bf16[2,512,256]{2,1,0:T(8,128)(2,1)} %reshape.26.kv, ...), custom_call_target="tpu_custom_call" | custom-call | tf_op jit(solution)/shard_map/pallas_call | solution.py:488
  129.7 0.0 copy-start.1
  129.7 2.3 %copy.15 = bf16[1,256,2048]{2,1,0:T(8,128)(2,1)} copy(bf16[1,256,2048]{2,1,0:T(8,128)(2,1)} %bitcast.12) | data formatting | bytes 2097152
  132.0 0.0 copy-done.1
  132.0 0.7 copy.16
  (1 shorter events, 0.0 us)
Async XLA Ops:
  0.6 2.7 %copy-start = (bf16[512,2,256]{2,1,0:T(2,128)(2,1)S(1)}, bf16[512,2,256]{2,1,0:T(2,128)(2,1)}, u32[]{:S(2)}) copy-start(bf16[512,2,256]{2,1,0:T(2,128)(2,1)} %param.8) | copy-start | bytes 1572868
  129.7 2.4 %copy-start.1 = (bf16[8,128,128]{2,1,0:T(8,128)(2,1)S(1)}, bf16[8,128,128]{2,1,0:T(8,128)(2,1)}, u32[]{:S(2)}) copy-start(bf16[8,128,128]{2,1,0:T(8,128)(2,1)} %get-tuple-element.5) | copy-start | bytes 786436

commit v3 on v2

--- a/solution.py
+++ b/solution.py
@@ -311,15 +311,8 @@
         och.forward(s)
         return c
 
-    lax.fori_loop(2, links, rest, 0)
-
-    def await_o(a, c):
-        @pl.when(a != z)
-        def _():
-            och.arrive(a)
-        return c
-
-    lax.fori_loop(0, links, await_o, 0)
+    lax.fori_loop(2, links - homes + 1, rest, 0)
+
     def project(a, ref):
         value = None
         for g in range(groups):
@@ -332,29 +325,36 @@
         return rdma(dsend.at[i, side], drecv.at[i, side], ds.at[i, side], dr.at[i, side],
                     tensor=1 - t)
 
-    def away(side, ref):
-        def one(i, c):
-            dsend[i, side] = project((1 - t) * homes + i, ref)
-            swap(i, side).start()
-            return c
-        lax.fori_loop(0, homes, one, 0)
-
-    away(0, asend)
+    def give(i):
+        return rdma(xsend.at[i], xrecv.at[i], xs.at[i], xr.at[i], dp=mate)
+
+    def await_o(a):
+        @pl.when(a != z)
+        def _():
+            och.arrive(a)
+
     for g in range(groups):
         attended(g).wait_recv()
-    away(1, arecv)
-
-    def give(i):
-        return rdma(xsend.at[i], xrecv.at[i], xs.at[i], xr.at[i], dp=mate)
-
-    def theirs(i, c):
-        value = project(t * homes + i, arecv)
+
+    def blocks(k, c):
+        @pl.when(k > 0)
+        def _():
+            och.forward(links - homes + k)
+        i = jnp.where(z >= homes, homes - 1 - k, k)
+        far, near = (1 - t) * homes + i, t * homes + i
+        await_o(far)
+        dsend[i, 1] = project(far, arecv)
+        swap(i, 1).start()
+        await_o(near)
+        value = project(near, arecv)
         swap(i, 1).wait_recv()
         xsend[i] = (value + drecv[i, 1]).astype(BF16)
         give(i).start()
-        return c
-
-    lax.fori_loop(0, homes, theirs, 0)
+        dsend[i, 0] = project(far, asend)
+        swap(i, 0).start()
+        return c
+
+    lax.fori_loop(0, homes, blocks, 0)
 
     def wait_first(k, c):
         p = (me + k) % n

time: 133 us -> 129 us (0.970)
  Pallas kernels: 125 us -> 121 us
    pallas_call x1, Pallas kernels: 125 us -> 121 us  [on_device(): pl.pallas_call(functools.partial(kernel, n, groups, group), out_shape=(ja...]
where the time goes in v3:
time: 129 us
  Pallas kernels  121 us (94%)
  local copies, waits for them, and re-layouts  4.55 us (4%)
  between operations  2.02 us (2%)
  other arithmetic  1.35 us (1%)
    pallas_call x1, Pallas kernels, on_device(): pl.pallas_call(functools.partial(kernel, n, groups, group), out_shape=(ja...  121 us
    unnamed x6, local copies, waits for them, and re-layouts  3.06 us

profile of v3, /device:TPU:0, one launch (start us, length us, event | category | flops | bytes accessed | tf_op | source)
XLA Modules:
  0.0 129.0 jit_solution(17535520469704025279)
XLA Ops:
  0.6 0.0 copy-start
  2.0 0.5 fusion.2
  2.5 0.8 pad_maximum_fusion
  3.4 0.0 copy-done
  3.4 0.4 bitcast_bitcast_fusion
  3.7 1.1 reshape.26.kv
  4.9 121.0 %shard_map.77 = (bf16[256,2048]{1,0:T(8,128)(2,1)}, bf16[8,128,128]{2,1,0:T(8,128)(2,1)}) custom-call(s32[1]{0:T(128)S(6)} %copy.13.length_ref, s32[1]{0:T(128)S(6)} %copy.14.dest_ref, bf16[256,4096]{1,0:T(8,128)(2,1)} %bitcast.11, bf16[512,1024]{1,0:T(8,128)(2,1)} %q.1, bf16[2,512,256]{2,1,0:T(8,128)(2,1)} %reshape.26.kv, ...), custom_call_target="tpu_custom_call" | custom-call | tf_op jit(solution)/shard_map/pallas_call | solution.py:488
  125.9 0.0 copy-start.1
  125.9 2.3 %copy.15 = bf16[1,256,2048]{2,1,0:T(8,128)(2,1)} copy(bf16[1,256,2048]{2,1,0:T(8,128)(2,1)} %bitcast.12) | data formatting | bytes 2097152
  128.3 0.0 copy-done.1
  128.3 0.7 copy.16
  (1 shorter events, 0.0 us)
Async XLA Ops:
  0.6 2.7 %copy-start = (bf16[512,2,256]{2,1,0:T(2,128)(2,1)S(1)}, bf16[512,2,256]{2,1,0:T(2,128)(2,1)}, u32[]{:S(2)}) copy-start(bf16[512,2,256]{2,1,0:T(2,128)(2,1)} %param.8) | copy-start | bytes 1572868
  125.9 2.4 %copy-start.1 = (bf16[8,128,128]{2,1,0:T(8,128)(2,1)S(1)}, bf16[8,128,128]{2,1,0:T(8,128)(2,1)}, u32[]{:S(2)}) copy-start(bf16[8,128,128]{2,1,0:T(8,128)(2,1)} %get-tuple-element.5) | copy-start | bytes 786436
